TPU v7x, 32 devices: a whole 2x2x4 slice. The times are simulated.
32 devices in a mesh: sp: 4 (over x, core), tp: 8 (over z, y).
Axes of the slice: x: 2, y: 2, z: 4, core: 2. Of those that a mesh axis runs over, the one named last changes fastest.
Arguments:
- tokens: bfloat16 [8, 220, 4096], P(None, 'sp'), may hold values from -6 to 6
- modulation: float32 [6, 4096], replicated, may hold values from -2.5 to 2.5
- w_qkv: bfloat16 [4096, 3, 4096], P('sp', None, 'tp'), may hold values from -4 to 4
- w_out: bfloat16 [4096, 4096], P('tp', 'sp'), may hold values from -0.09375 to 0.09375
- w_up: bfloat16 [4096, 16384], P('sp', 'tp'), may hold values from -0.09375 to 0.09375
- w_down: bfloat16 [16384, 4096], P('tp', 'sp'), may hold values from -0.046875 to 0.046875
Outputs:
- block_out: bfloat16 [8, 220, 4096], P(None, 'sp', 'tp')
All inputs are finite; a program needn't handle non-finite values.
Results may differ from a plain program's by a relative error of at most 0.012.
Values may be sent and summed in bfloat16 or wider, within the bound.
No kernel may reach another device: no remote copies, remote signals or barrier semaphores. Data moves between devices by JAX's collectives and lax.ppermute only.
A program may use at most 128 MiB of HBM per device.

v0:
```python
import jax
import jax.numpy as jnp
from jax import lax
from jax.sharding import PartitionSpec as P

DH = 128
EPSILON = 1e-06


def normalize(tok_rows, shift_vec, scale_vec):
    values = tok_rows.astype(jnp.float32)
    center = jnp.mean(values, axis=-1, keepdims=True)
    spread = jnp.mean(jnp.square(values - center), axis=-1, keepdims=True)
    scaled = (values - center) * lax.rsqrt(spread + EPSILON)
    return (scaled * (1.0 + scale_vec) + shift_vec).astype(jnp.bfloat16)


def project_rows(operand, weight, einsum_form):
    return jnp.einsum(
        einsum_form,
        operand,
        lax.all_gather(weight, "sp", axis=0, tiled=True),
        preferred_element_type=jnp.float32,
    )


def project_cols(operand, weight, einsum_form, leading):
    portion = lax.all_gather(weight, "sp", axis=1, tiled=True)
    shaped = portion.reshape(leading + (portion.shape[1],))
    return jnp.einsum(einsum_form, operand, shaped, preferred_element_type=jnp.float32)


def attend_items(pieces):
    queries, key_rows, values = pieces
    factor = queries.shape[-1] ** (-0.5)

    def single(triple):
        query_one, key_one, value_one = triple
        scores = (
            lax.dot_general(
                query_one, key_one, (((1,), (1,)), ((), ())), preferred_element_type=jnp.float32
            )
            * factor
        )
        row_max = jnp.max(scores, axis=1, keepdims=True)
        raw_weights = jnp.exp(scores - row_max)
        att_weights = (raw_weights / jnp.sum(raw_weights, axis=1, keepdims=True)).astype(
            jnp.bfloat16
        )
        return jnp.dot(att_weights, value_one, preferred_element_type=jnp.float32).astype(
            jnp.bfloat16
        )

    result = lax.map(single, (queries[0], key_rows[0], values[0]))
    return result[None]


def attention_combine(base, partial_value, gate):
    summed = lax.psum(partial_value.astype(jnp.bfloat16), "tp").astype(jnp.float32)
    full = (base.astype(jnp.float32) + gate * summed).astype(jnp.bfloat16)
    return full


def mlp_combine(base, partial_value, gate):
    tp_count = lax.axis_size("tp")
    width = base.shape[2] // tp_count
    offset = lax.axis_index("tp") * width
    base_mine = lax.dynamic_slice_in_dim(base, offset, width, 2).astype(jnp.float32)
    gate_mine = lax.dynamic_slice_in_dim(gate, offset, width, 0)
    share = lax.psum_scatter(
        partial_value.astype(jnp.bfloat16), "tp", scatter_dimension=2, tiled=True
    ).astype(jnp.float32)
    return (base_mine + gate_mine * share).astype(jnp.bfloat16)


def shards(tokens, modulation, w_qkv, w_out, w_up, w_down):
    frames, patches, width = tokens.shape
    heads_local = w_qkv.shape[2] // DH
    sp_count = lax.axis_size("sp")
    items_dev = heads_local * frames // sp_count
    mod_a = normalize(tokens, modulation[0], modulation[1])
    weight_qkv = w_qkv.reshape(w_qkv.shape[0], 3, heads_local, DH)
    projected = project_rows(mod_a, weight_qkv, "fpd,dshe->shfpe").astype(jnp.bfloat16)
    projected = projected.reshape(3, sp_count, items_dev, patches, DH)
    attended = attend_items(
        (
            lax.all_to_all(projected[0], "sp", split_axis=0, concat_axis=2, tiled=True),
            lax.all_to_all(projected[1], "sp", split_axis=0, concat_axis=2, tiled=True),
            lax.all_to_all(projected[2], "sp", split_axis=0, concat_axis=2, tiled=True),
        )
    )
    returned = lax.all_to_all(attended, "sp", split_axis=2, concat_axis=0, tiled=True)
    returned = returned.reshape(heads_local, frames, patches, DH)
    partial_attn = project_cols(returned, w_out, "hfpd,hde->fpe", (heads_local, DH))
    middle = attention_combine(tokens, partial_attn, modulation[2])
    mod_b = normalize(middle, modulation[3], modulation[4])
    up_proj = project_rows(mod_b, w_up, "fpd,dc->fpc")
    hidden = jax.nn.gelu(up_proj, approximate=True).astype(jnp.bfloat16)
    partial_mlp = project_cols(hidden, w_down, "fpk,kc->fpc", (w_down.shape[0],))
    return mlp_combine(middle, partial_mlp, modulation[5])


def solution(mesh):
    placed = (
        P(None, "sp", None),
        P(),
        P("sp", None, "tp"),
        P("tp", "sp"),
        P("sp", "tp"),
        P("tp", "sp"),
    )
    return jax.shard_map(
        shards, mesh=mesh, in_specs=placed, out_specs=P(None, "sp", "tp"), check_vma=False
    )
```

profile of v0, /device:TPU:0, one launch (start us, length us, event | category | flops | bytes accessed | tf_op | source)
XLA Modules:
  0.0 655.9 jit_solution(7131236097919553995)
XLA Ops:
  6.5 3.2 copy.22
  9.7 2.8 copy.23
  12.6 0.7 all-gather.7.cloned.1.call-update
  13.4 5.8 convert_reduce_fusion
  19.2 3.9 fusion.23
  23.1 74.4 %all-gather.5.cloned.1.call-done = bf16[4096,3,4,128]{3,0,2,1:T(8,128)(2,1)} async-done(((bf16[1024,3,4,128]{3,0,2,1:T(8,128)(2,1)}), bf16[4096,3,4,128]{3,0,2,1:T(8,128)(2,1)}) %all-gather.5.cloned.1.call-update) | async-done | bytes 12582928 | tf_op jit(solution)/shard_map/all_gather | solution.py:22
  97.5 18.3 %fusion.69 = bf16[3,4,8,55,128]{4,3,1,0,2:T(8,128)(2,1)S(1)} fusion(bf16[4096,3,4,128]{3,0,2,1:T(8,128)(2,1)} %all-gather.5.cloned.1.call-done, f32[4096]{0:T(1024)S(1)} %bitcast.107, f32[4096]{0:T(1024)S(1)} %bitcast.108, f32[8,55]{1,0:T(8,128)S(1)} %add_rsqrt_fusion.1, f32[8,55]{1,0:T(8,128)S(1)} %broadcast_multiply_fusion.1, bf16[8,55,4096]{2,0,1:T(8,128)(2,1)} %param.8), kind=kOutput, calls=%fused_computation.64 | convolution fusion | flops 5547970560 | bytes 17575360 | tf_op jit(solution)/shard_map/fpd,dshe->shfpe/dot_general | solution.py:19
  115.9 0.9 copy.24
  116.9 3.5 all-to-all-start
  120.3 0.9 copy.25
  121.3 12.3 %all-to-all-done = bf16[4,8,55,128]{3,1,2,0:T(8,128)(2,1)S(1)} async-done(((bf16[4,8,55,128]{3,1,2,0:T(8,128)(2,1)}), bf16[4,8,55,128]{3,1,2,0:T(8,128)(2,1)S(1)}, u32[]{:S(2)}, u32[]{:S(2)}) %all-to-all-start) | async-done | bytes 450592 | tf_op jit(solution)/shard_map/all_to_all | solution.py:87
  133.6 3.5 all-to-all-start.1
  137.1 0.9 copy.26
  138.0 7.0 %all-to-all-done.1 = bf16[4,8,55,128]{3,1,2,0:T(8,128)(2,1)S(1)} async-done(((bf16[4,8,55,128]{3,1,2,0:T(8,128)(2,1)}), bf16[4,8,55,128]{3,1,2,0:T(8,128)(2,1)S(1)}, u32[]{:S(2)}, u32[]{:S(2)}) %all-to-all-start.1) | async-done | bytes 450592 | tf_op jit(solution)/shard_map/all_to_all | solution.py:88
  145.0 3.5 all-to-all-start.2
  148.7 7.8 %all-to-all-done.2 = bf16[4,8,55,128]{3,1,2,0:T(8,128)(2,1)S(1)} async-done(((bf16[4,8,55,128]{3,1,2,0:T(8,128)(2,1)}), bf16[4,8,55,128]{3,1,2,0:T(8,128)(2,1)S(1)}, u32[]{:S(2)}, u32[]{:S(2)}) %all-to-all-start.2) | async-done | bytes 450592 | tf_op jit(solution)/shard_map/all_to_all | solution.py:89
  156.6 4.6 while.10
  161.2 0.9 copy.52
  162.1 3.5 all-to-all-start.3
  165.6 7.9 %all-to-all-done.3 = bf16[1,8,220,128]{3,1,0,2:T(8,128)(2,1)S(1)} async-done(((bf16[1,8,220,128]{3,1,0,2:T(8,128)(2,1)}), bf16[1,8,220,128]{3,1,0,2:T(8,128)(2,1)S(1)}, u32[]{:S(2)}, u32[]{:S(2)}) %all-to-all-start.3) | async-done | bytes 450592 | tf_op jit(solution)/shard_map/all_to_all | solution.py:92
  173.6 5.7 bitcast_convert_fusion
  180.0 0.5 all-gather.9.cloned.1.call-update
  180.8 141.6 %all-reduce.2.cloned.1.call-done = bf16[8,55,4096]{2,1,0:T(8,128)(2,1)} async-done(((bf16[8,55,4096]{2,1,0:T(8,128)(2,1)}), bf16[8,55,4096]{2,1,0:T(8,128)(2,1)}) %all-reduce.2.cloned.1.call-update) | async-done | bytes 3604496 | tf_op jit(solution)/shard_map/psum | solution.py:59
  322.4 8.3 %convert_reduce_fusion.1 = (f32[8,55]{1,0:T(8,128)S(1)}, bf16[8,55,4096]{2,1,0:T(8,128)(2,1)S(1)}) fusion(bf16[8,55,4096]{2,1,0:T(8,128)(2,1)} %all-reduce.2.cloned.1.call-done, f32[4096]{0:T(1024)S(1)} %bitcast.104, bf16[8,55,4096]{2,0,1:T(8,128)(2,1)} %param.8), kind=kLoop, calls=%fused_computation.27 | loop fusion | flops 12615240 | bytes 10831584 | tf_op jit(solution)/shard_map/reduce_sum | solution.py:12
  330.7 2.0 copy-done.1
  332.7 1.1 fusion.27
  333.8 94.7 %all-gather.11.cloned.1.call-done = bf16[2048,4096]{1,0:T(8,128)(2,1)} async-done(((bf16[2048,1024]{1,0:T(8,128)(2,1)}), bf16[2048,4096]{1,0:T(8,128)(2,1)}) %all-gather.11.cloned.1.call-update) | async-done | bytes 16777232 | tf_op jit(solution)/shard_map/all_gather | solution.py:28
  428.5 107.3 %all-gather.9.cloned.1.call-done = bf16[4096,2048]{1,0:T(8,128)(2,1)} async-done(((bf16[1024,2048]{1,0:T(8,128)(2,1)}), bf16[4096,2048]{1,0:T(8,128)(2,1)}) %all-gather.9.cloned.1.call-update) | async-done | bytes 16777232 | tf_op jit(solution)/shard_map/all_gather | solution.py:22
  535.9 29.4 %fusion.32 = bf16[8,55,4096]{2,1,0:T(8,128)(2,1)} fusion(bf16[2048,4096]{1,0:T(8,128)(2,1)} %all-gather.11.cloned.1.call-done, bf16[4096,2048]{1,0:T(8,128)(2,1)} %all-gather.9.cloned.1.call-done, bf16[8,55,4096]{2,1,0:T(8,128)(2,1)} %copy-done.1, f32[4096]{0:T(1024)S(1)} %bitcast.105, f32[4096]{0:T(1024)S(1)} %bitcast.106, f32[8,55]{1,0:T(8,128)S(1)} %add_rsqrt_fusion, ...), kind=kOutput, calls=%fused_computation.42 | convolution fusion | flops 14784675840 | bytes 40799680 | tf_op jit(solution)/shard_map/fpk,kc->fpc/dot_general | solution.py:30
  565.4 81.5 %reduce-scatter.2.cloned.1.call-done = bf16[8,55,512]{2,1,0:T(8,128)(2,1)} async-done(((bf16[8,55,4096]{2,1,0:T(8,128)(2,1)}), bf16[8,55,512]{2,1,0:T(8,128)(2,1)}) %reduce-scatter.2.cloned.1.call-update) | async-done | bytes 450576 | tf_op jit(solution)/shard_map/reduce_scatter | solution.py:70
  646.9 1.3 add_convert_fusion
  648.2 0.9 copy.32
  (51 shorter events, 5.9 us)
Async XLA Ops:
  6.5 91.0 %all-gather.5.cloned.1.call-start = ((), (), s32[]{:S(2)}) async-start(), calls=%async_computation.5 | async-start | bytes 15728640 | tf_op jit(solution)/shard_map/all_gather | solution.py:22
  9.7 3.6 copy-start.2
  12.6 153.1 %all-gather.7.cloned.1.call-start = ((), (), s32[]{:S(2)}) async-start(), calls=%async_computation.6 | async-start | bytes 5242880 | tf_op jit(solution)/shard_map/all_gather | solution.py:28
  13.3 5.9 copy-start
  116.9 16.7 %all-to-all-start = ((bf16[4,8,55,128]{3,1,2,0:T(8,128)(2,1)}), bf16[4,8,55,128]{3,1,2,0:T(8,128)(2,1)S(1)}, u32[]{:S(2)}, u32[]{:S(2)}) async-start(bf16[4,8,55,128]{3,1,2,0:T(8,128)(2,1)} %copy.24), calls=%async_computation | async-start | bytes 901120 | tf_op jit(solution)/shard_map/all_to_all | solution.py:87
  133.6 11.5 %all-to-all-start.1 = ((bf16[4,8,55,128]{3,1,2,0:T(8,128)(2,1)}), bf16[4,8,55,128]{3,1,2,0:T(8,128)(2,1)S(1)}, u32[]{:S(2)}, u32[]{:S(2)}) async-start(bf16[4,8,55,128]{3,1,2,0:T(8,128)(2,1)} %copy.25), calls=%async_computation.1 | async-start | bytes 901120 | tf_op jit(solution)/shard_map/all_to_all | solution.py:88
  145.0 11.5 %all-to-all-start.2 = ((bf16[4,8,55,128]{3,1,2,0:T(8,128)(2,1)}), bf16[4,8,55,128]{3,1,2,0:T(8,128)(2,1)S(1)}, u32[]{:S(2)}, u32[]{:S(2)}) async-start(bf16[4,8,55,128]{3,1,2,0:T(8,128)(2,1)} %copy.26), calls=%async_computation.2 | async-start | bytes 901120 | tf_op jit(solution)/shard_map/all_to_all | solution.py:89
  162.1 11.5 %all-to-all-start.3 = ((bf16[1,8,220,128]{3,1,0,2:T(8,128)(2,1)}), bf16[1,8,220,128]{3,1,0,2:T(8,128)(2,1)S(1)}, u32[]{:S(2)}, u32[]{:S(2)}) async-start(bf16[1,8,220,128]{3,1,0,2:T(8,128)(2,1)} %bitcast.90), calls=%async_computation.3 | async-start | bytes 901120 | tf_op jit(solution)/shard_map/all_to_all | solution.py:92
  165.6 156.8 %all-reduce.2.cloned.1.call-start = ((), (), s32[]{:S(2)}) async-start(), calls=%async_computation.7 | async-start | bytes 7340032 | tf_op jit(solution)/shard_map/psum | solution.py:59
  179.3 249.2 %all-gather.11.cloned.1.call-start = ((), (), s32[]{:S(2)}) async-start(), calls=%async_computation.9 | async-start | bytes 20971520 | tf_op jit(solution)/shard_map/all_gather | solution.py:28
  179.9 356.0 %all-gather.9.cloned.1.call-start = ((), (), s32[]{:S(2)}) async-start(), calls=%async_computation.8 | async-start | bytes 20971520 | tf_op jit(solution)/shard_map/all_gather | solution.py:22
  180.5 466.4 %reduce-scatter.2.cloned.1.call-start = ((), (), s32[]{:S(2)}) async-start(), calls=%async_computation.10 | async-start | bytes 4128768 | tf_op jit(solution)/shard_map/reduce_scatter | solution.py:70
  330.7 2.0 copy-start.1
Sparse Core Ops, SparseCore 0:
  12.7 84.7 all-gather.4
  99.1 39.4 all-gather.6
  179.4 142.8 all-reduce.1
  323.8 104.7 all-gather.10
  429.9 105.8 all-gather.8
  565.5 81.3 reduce-scatter.1
where the time goes:
time: 656 us
  waiting for transfers between devices  536 us (82%)
  matrix products  57.3 us (9%)
  other arithmetic  21.1 us (3%)
  starting transfers between devices  14.3 us (2%)
  between operations  13.6 us (2%)
  local copies, waits for them, and re-layouts  13 us (2%)
    all_gather x2, waiting for transfers between devices, project_rows(): lax.all_gather(weight, 'sp', axis=0, tiled=True)  182 us
    psum x1, waiting for transfers between devices, attention_combine(): lax.psum(partial_value.astype(jnp.bfloat16), 'tp').astype(jnp.float32)  142 us
    all_gather x2, waiting for transfers between devices, project_cols(): portion = lax.all_gather(weight, 'sp', axis=1, tiled=True)  94.7 us
    reduce_scatter x1, waiting for transfers between devices, mlp_combine(): lax.psum_scatter(partial_value.astype(jnp.bfloat16), 'tp', scatter_dimens...  81.5 us
    dot_general x2, matrix products, project_cols(): jnp.einsum(einsum_form, operand, shaped, preferred_element_type=jnp.float32)  35.2 us
    dot_general x1, matrix products, project_rows(): jnp.einsum(einsum_form, operand, lax.all_gather(weight, 'sp', axis=0, til...  18.3 us
    reduce_sum x2, other arithmetic, normalize(): center = jnp.mean(values, axis=-1, keepdims=True)  14.1 us
  transfers between devices with their start and end apart: 10, of which 9 were waited for; matrix products, arithmetic and copies ran while one was open for 7% of the time, Pallas kernels for 0%

commit v1 on v0

--- a/solution.py
+++ b/solution.py
@@ -25,7 +25,12 @@
 
 
 def project_cols(operand, weight, einsum_form, leading):
-    portion = lax.all_gather(weight, "sp", axis=1, tiled=True)
+    ring = [weight]
+    for hop in range(3):
+        ring.append(lax.ppermute(ring[-1], "sp", [(dev, (dev + 1) % 4) for dev in range(4)]))
+    portion = jnp.roll(
+        jnp.concatenate(ring[::-1], axis=1), (lax.axis_index("sp") + 1) * ring[0].shape[1], axis=1
+    )
     shaped = portion.reshape(leading + (portion.shape[1],))
     return jnp.einsum(einsum_form, operand, shaped, preferred_element_type=jnp.float32)
 

time: 656 us -> 581 us (0.89); the launches traced: 656 us -> 573 us
  waiting for transfers between devices: 536 us -> 398 us
  local copies, waits for them, and re-layouts: 13 us -> 56.4 us
  starting transfers between devices: 14.3 us -> 23.2 us
    ppermute x0 -> x6, waiting for transfers between devices: none -> 181 us  [project_cols(): lax.ppermute(ring[-1], 'sp', [(dev, (dev + 1) % 4) for dev in range(4)])]
    psum x1, waiting for transfers between devices: 142 us -> 0.01 us  [attention_combine(): lax.psum(partial_value.astype(jnp.bfloat16), 'tp').astype(jnp.float32)]
    all_gather x2 -> x0, waiting for transfers between devices: 94.7 us -> none  [project_cols(): portion = lax.all_gather(weight, 'sp', axis=1, tiled=True)]
    all_gather x2, waiting for transfers between devices: 182 us -> 125 us  [project_rows(): lax.all_gather(weight, 'sp', axis=0, tiled=True)]
    unnamed x7 -> x23, local copies, waits for them, and re-layouts: 5.18 us -> 33.4 us
    dot_general x2, matrix products: 35.2 us -> 18.5 us  [project_cols(): jnp.einsum(einsum_form, operand, shaped, preferred_element_type=jnp.float32)]
    dot_general x1 -> x2, matrix products: 18.3 us -> 31.9 us  [project_rows(): jnp.einsum(einsum_form, operand, lax.all_gather(weight, 'sp', axis=0, til...]
    all_to_all x1, waiting for transfers between devices: 12.3 us -> 2.67 us  [shards(): lax.all_to_all(projected[0], 'sp', split_axis=0, concat_axis=2, tiled=True)]
  transfers between devices with their start and end apart: 10 -> 14, of which waited for: 9 -> 12; matrix products, arithmetic and copies ran while one was open for 7% -> 15% of each run, Pallas kernels for 0% -> 0%
where the time goes in v1:
time: 581 us; the launch traced here: 573 us
  waiting for transfers between devices  398 us (69%)
  matrix products  59.2 us (10%)
  local copies, waits for them, and re-layouts  56.4 us (10%)
  starting transfers between devices  23.2 us (4%)
  other arithmetic  22.8 us (4%)
  between operations  13.6 us (2%)
    ppermute x6, waiting for transfers between devices, project_cols(): lax.ppermute(ring[-1], 'sp', [(dev, (dev + 1) % 4) for dev in range(4)])  181 us
    all_gather x2, waiting for transfers between devices, project_rows(): lax.all_gather(weight, 'sp', axis=0, tiled=True)  125 us
    reduce_scatter x1, waiting for transfers between devices, mlp_combine(): lax.psum_scatter(partial_value.astype(jnp.bfloat16), 'tp', scatter_dimens...  81.5 us
    unnamed x23, local copies, waits for them, and re-layouts  33.4 us
    dot_general x2, matrix products, project_rows(): jnp.einsum(einsum_form, operand, lax.all_gather(weight, 'sp', axis=0, til...  31.9 us
    dot_general x2, matrix products, project_cols(): jnp.einsum(einsum_form, operand, shaped, preferred_element_type=jnp.float32)  18.5 us
    reduce_sum x2, other arithmetic, normalize(): center = jnp.mean(values, axis=-1, keepdims=True)  13.8 us
  transfers between devices with their start and end apart: 14, of which 12 were waited for; matrix products, arithmetic and copies ran while one was open for 15% of the time, Pallas kernels for 0%

profile of v1, /device:TPU:0, one launch (start us, length us, event | category | flops | bytes accessed | tf_op | source)
XLA Modules:
  0.0 573.4 jit_solution(4964862241632153725)
XLA Ops:
  6.5 3.2 copy.22
  9.7 2.8 copy.23
  13.1 5.6 convert_reduce_fusion
  18.8 5.9 %fusion.24 = f32[8,55]{1,0:T(8,128)S(1)} fusion(f32[8,55]{1,0:T(8,128)S(1)} %broadcast_multiply_fusion.1, bf16[8,55,4096]{2,0,1:T(8,128)(2,1)} %param.8), kind=kLoop, calls=%fused_computation.33 | loop fusion | flops 7208520 | bytes 3608000 | tf_op jit(solution)/shard_map/reduce_sum | solution.py:13
  24.7 3.1 collective-permute-done
  27.7 3.1 collective-permute-start.1
  30.9 33.6 %collective-permute-done.1 = bf16[512,1024]{1,0:T(8,128)(2,1)S(1)} collective-permute-done((bf16[512,1024]{1,0:T(8,128)(2,1)S(1)}, bf16[512,1024]{1,0:T(8,128)(2,1)S(1)}, u32[]{:S(2)}, u32[]{:S(2)}) %collective-permute-start.1) | collective-permute-done | bytes 1048608 | tf_op jit(solution)/shard_map/ppermute | solution.py:30
  64.6 3.4 collective-permute-start.2
  68.0 52.0 %all-gather.3.cloned.1.call-done = bf16[4096,3,4,128]{3,0,2,1:T(8,128)(2,1)} async-done(((bf16[1024,3,4,128]{3,0,2,1:T(8,128)(2,1)}), bf16[4096,3,4,128]{3,0,2,1:T(8,128)(2,1)}) %all-gather.3.cloned.1.call-update) | async-done | bytes 12582928 | tf_op jit(solution)/shard_map/all_gather | solution.py:22
  120.0 18.2 %fusion.65 = bf16[3,4,8,55,128]{4,3,1,0,2:T(8,128)(2,1)S(1)} fusion(bf16[4096,3,4,128]{3,0,2,1:T(8,128)(2,1)} %all-gather.3.cloned.1.call-done, f32[4096]{0:T(1024)S(1)} %bitcast.104, f32[4096]{0:T(1024)S(1)} %bitcast.105, f32[8,55]{1,0:T(8,128)S(1)} %add_rsqrt_fusion.1, f32[8,55]{1,0:T(8,128)S(1)} %broadcast_multiply_fusion.1, bf16[8,55,4096]{2,0,1:T(8,128)(2,1)} %param.8), kind=kOutput, calls=%fused_computation.64 | convolution fusion | flops 5547970560 | bytes 17575360 | tf_op jit(solution)/shard_map/fpd,dshe->shfpe/dot_general | solution.py:19
  140.3 4.1 all-to-all-start.2
  149.8 2.7 all-to-all-done.2
  152.5 4.1 all-to-all-start.1
  164.8 4.1 all-to-all-start
  174.3 2.7 all-to-all-done
  178.1 9.4 %while.10 = (s32[]{:T(128)}, bf16[8,220,128]{2,1,0:T(8,128)(2,1)}, bf16[8,220,128]{2,1,0:T(8,128)(2,1)S(1)}, bf16[8,220,128]{2,1,0:T(8,128)(2,1)S(1)}, bf16[8,220,128]{2,1,0:T(8,128)(2,1)S(1)}, /*index=5*/s32[]{:T(128)}) while((s32[]{:T(128)}, bf16[8,220,128]{2,1,0:T(8,128)(2,1)}, bf16[8,220,128]{2,1,0:T(8,128)(2,1)S(1)}, ...), condition=%wide.region_5.6_spmd, body=%wide.region_2.5_spmd.sunk | while | flops 25147320 | bytes 852765 | solution.py:59
  189.4 3.5 all-to-all-start.3
  192.9 4.7 constant_dynamic-slice_fusion.1
  197.6 3.3 all-to-all-done.3
  200.8 5.8 %bitcast_convert_fusion = bf16[8,55,4096]{2,1,0:T(8,128)(2,1)} fusion(bf16[4,128,4096,1]{2,1,0,3:T(8,128)(2,1)} %bitcast.99, bf16[1,8,4,55,128]{4,1,3,2,0:T(8,128)(2,1)S(1)} %bitcast.100), kind=kOutput, calls=%fused_computation.42 | convolution fusion | flops 1847296000 | bytes 8249344 | tf_op jit(solution)/shard_map/hfpd,hde->fpe/dot_general | solution.py:35
  207.5 48.1 %collective-permute-done.3 = bf16[2048,1024]{1,0:T(8,128)(2,1)S(1)} collective-permute-done((bf16[2048,1024]{1,0:T(8,128)(2,1)}, bf16[2048,1024]{1,0:T(8,128)(2,1)S(1)}, u32[]{:S(2)}, u32[]{:S(2)}) %collective-permute-start.3) | collective-permute-done | bytes 4194336 | tf_op jit(solution)/shard_map/ppermute | solution.py:30
  255.6 47.9 %collective-permute-done.4 = bf16[2048,1024]{1,0:T(8,128)(2,1)S(1)} collective-permute-done((bf16[2048,1024]{1,0:T(8,128)(2,1)S(1)}, bf16[2048,1024]{1,0:T(8,128)(2,1)S(1)}, u32[]{:S(2)}, u32[]{:S(2)}) %collective-permute-start.4) | collective-permute-done | bytes 4194336 | tf_op jit(solution)/shard_map/ppermute | solution.py:30
  303.7 47.9 %collective-permute-done.5 = bf16[2048,1024]{1,0:T(8,128)(2,1)S(1)} collective-permute-done((bf16[2048,1024]{1,0:T(8,128)(2,1)S(1)}, bf16[2048,1024]{1,0:T(8,128)(2,1)S(1)}, u32[]{:S(2)}, u32[]{:S(2)}) %collective-permute-start.5) | collective-permute-done | bytes 4194336 | tf_op jit(solution)/shard_map/ppermute | solution.py:30
  354.0 2.6 constant_dynamic-update-slice_fusion.14
  356.6 2.6 constant_dynamic-update-slice_fusion.13
  359.2 2.7 constant_dynamic-update-slice_fusion.12
  364.4 3.2 constant_dynamic-update-slice_fusion.10
  372.3 8.2 %convert_reduce_fusion.1 = (f32[8,55]{1,0:T(8,128)S(1)}, bf16[8,55,4096]{2,1,0:T(8,128)(2,1)S(1)}) fusion(bf16[8,55,4096]{2,1,0:T(8,128)(2,1)} %all-reduce.2.cloned.1.call-done, f32[4096]{0:T(1024)S(1)} %bitcast.101, bf16[8,55,4096]{2,0,1:T(8,128)(2,1)} %param.8), kind=kLoop, calls=%fused_computation.28 | loop fusion | flops 12615240 | bytes 10831584 | tf_op jit(solution)/shard_map/reduce_sum | solution.py:12
  383.6 72.9 %all-gather.5.cloned.1.call-done = bf16[4096,2048]{1,0:T(8,128)(2,1)} async-done(((bf16[1024,2048]{1,0:T(8,128)(2,1)}), bf16[4096,2048]{1,0:T(8,128)(2,1)}) %all-gather.5.cloned.1.call-update) | async-done | bytes 16777232 | tf_op jit(solution)/shard_map/all_gather | solution.py:22
  456.5 13.7 %fusion.43 = bf16[8,55,2048]{2,1,0:T(8,128)(2,1)S(1)} fusion(bf16[4096,2048]{1,0:T(8,128)(2,1)} %all-gather.5.cloned.1.call-done, bf16[8,55,4096]{2,1,0:T(8,128)(2,1)} %copy-done.1, f32[4096]{0:T(1024)S(1)} %bitcast.102, f32[4096]{0:T(1024)S(1)} %bitcast.103, f32[8,55]{1,0:T(8,128)S(1)} %add_rsqrt_fusion, f32[8,55]{1,0:T(8,128)S(1)} %broadcast_multiply_fusion), kind=kOutput, calls=%fused_computation.52 | convolution fusion | flops 7400898560 | bytes 22220224 | tf_op jit(solution)/shard_map/fpd,dc->fpc/dot_general | solution.py:19
  470.2 12.7 %fusion.33 = bf16[8,55,4096]{2,1,0:T(8,128)(2,1)} fusion(bf16[8,55,2048]{2,1,0:T(8,128)(2,1)S(1)} %fusion.43, bf16[2048,8192]{1,0:T(8,128)(2,1)} %constant_dynamic-update-slice_fusion.8, s32[]{:T(128)S(6)} %select_n.24), kind=kOutput, calls=%fused_computation.43 | convolution fusion | flops 7383777280 | bytes 22183940 | tf_op jit(solution)/shard_map/fpk,kc->fpc/dot_general | solution.py:35
  482.9 81.5 %reduce-scatter.2.cloned.1.call-done = bf16[8,55,512]{2,1,0:T(8,128)(2,1)} async-done(((bf16[8,55,4096]{2,1,0:T(8,128)(2,1)}), bf16[8,55,512]{2,1,0:T(8,128)(2,1)}) %reduce-scatter.2.cloned.1.call-update) | async-done | bytes 450576 | tf_op jit(solution)/shard_map/reduce_scatter | solution.py:75
  (77 shorter events, 49.7 us)
Async XLA Ops:
  6.5 113.5 %all-gather.3.cloned.1.call-start = ((), (), s32[]{:S(2)}) async-start(), calls=%async_computation.5 | async-start | bytes 15728640 | tf_op jit(solution)/shard_map/all_gather | solution.py:22
  9.7 21.1 %copy-start.3 = (f32[6,4096]{1,0:T(8,128)S(1)}, f32[6,4096]{1,0:T(8,128)}, u32[]{:S(2)}) copy-start(f32[6,4096]{1,0:T(8,128)} %param.9) | copy-start | bytes 294916
  12.6 15.2 %collective-permute-start = (bf16[512,1024]{1,0:T(8,128)(2,1)}, bf16[512,1024]{1,0:T(8,128)(2,1)S(1)}, u32[]{:S(2)}, u32[]{:S(2)}) collective-permute-start(bf16[512,1024]{1,0:T(8,128)(2,1)} %param.11), channel_id=1, source_target_pairs={{0,8},{8,16},{16,24},{24,0},{1,9},{9,17},{17,25},{25,1},{2,10},{10... | collective-permute-start | bytes 3145736 | tf_op jit(solution)/shard_map/ppermute | solution.py:30
  27.7 36.8 %collective-permute-start.1 = (bf16[512,1024]{1,0:T(8,128)(2,1)S(1)}, bf16[512,1024]{1,0:T(8,128)(2,1)S(1)}, u32[]{:S(2)}, u32[]{:S(2)}) collective-permute-start(bf16[512,1024]{1,0:T(8,128)(2,1)S(1)} %collective-permute-done), channel_id=1, source_target_pairs={{0,8},{8,16},{16,24},{24,0},{1,9},{9,17},{17,25},{25,1},{2,10},{10... | collective-permute-start | bytes 3145736 | tf_op jit(solution)/shard_map/ppermute | solution.py:30
  64.6 79.9 %collective-permute-start.2 = (bf16[512,1024]{1,0:T(8,128)(2,1)S(1)}, bf16[512,1024]{1,0:T(8,128)(2,1)}, u32[]{:S(2)}, u32[]{:S(2)}) collective-permute-start(bf16[512,1024]{1,0:T(8,128)(2,1)S(1)} %collective-permute-done.1), channel_id=1, source_target_pairs={{0,8},{8,16},{16,24},{24,0},{1,9},{9,17},{17,25},{25,1},{2,10},{10... | collective-permute-start | bytes 3145736 | tf_op jit(solution)/shard_map/ppermute | solution.py:30
  138.3 19.5 %copy-start.2 = (bf16[512,1024]{1,0:T(8,128)(2,1)S(1)}, bf16[512,1024]{1,0:T(8,128)(2,1)}, u32[]{:S(2)}) copy-start(bf16[512,1024]{1,0:T(8,128)(2,1)} %param.11) | copy-start | bytes 3145732
  140.3 12.2 %all-to-all-start.2 = ((bf16[4,8,55,128]{3,1,2,0:T(8,128)(2,1)}), bf16[4,8,55,128]{3,1,2,0:T(8,128)(2,1)}, u32[]{:S(2)}, u32[]{:S(2)}) async-start(bf16[4,8,55,128]{3,1,2,0:T(8,128)(2,1)} %copy.26), calls=%async_computation.2 | async-start | bytes 901120 | tf_op jit(solution)/shard_map/all_to_all | solution.py:94
  152.5 12.2 %all-to-all-start.1 = ((bf16[4,8,55,128]{3,1,2,0:T(8,128)(2,1)}), bf16[4,8,55,128]{3,1,2,0:T(8,128)(2,1)}, u32[]{:S(2)}, u32[]{:S(2)}) async-start(bf16[4,8,55,128]{3,1,2,0:T(8,128)(2,1)} %copy.25), calls=%async_computation.1 | async-start | bytes 901120 | tf_op jit(solution)/shard_map/all_to_all | solution.py:93
  164.8 12.2 %all-to-all-start = ((bf16[4,8,55,128]{3,1,2,0:T(8,128)(2,1)}), bf16[4,8,55,128]{3,1,2,0:T(8,128)(2,1)}, u32[]{:S(2)}, u32[]{:S(2)}) async-start(bf16[4,8,55,128]{3,1,2,0:T(8,128)(2,1)} %copy.24), calls=%async_computation | async-start | bytes 901120 | tf_op jit(solution)/shard_map/all_to_all | solution.py:92
  189.4 11.5 %all-to-all-start.3 = ((bf16[1,8,220,128]{3,1,0,2:T(8,128)(2,1)}), bf16[1,8,220,128]{3,1,0,2:T(8,128)(2,1)S(1)}, u32[]{:S(2)}, u32[]{:S(2)}) async-start(bf16[1,8,220,128]{3,1,0,2:T(8,128)(2,1)} %bitcast.89), calls=%async_computation.3 | async-start | bytes 901120 | tf_op jit(solution)/shard_map/all_to_all | solution.py:97
  192.8 179.5 %all-reduce.2.cloned.1.call-start = ((), (), s32[]{:S(2)}) async-start(), calls=%async_computation.6 | async-start | bytes 7340032 | tf_op jit(solution)/shard_map/psum | solution.py:64
  206.6 249.9 %all-gather.5.cloned.1.call-start = ((), (), s32[]{:S(2)}) async-start(), calls=%async_computation.7 | async-start | bytes 20971520 | tf_op jit(solution)/shard_map/all_gather | solution.py:22
  207.4 357.1 %reduce-scatter.2.cloned.1.call-start = ((), (), s32[]{:S(2)}) async-start(), calls=%async_computation.8 | async-start | bytes 4128768 | tf_op jit(solution)/shard_map/reduce_scatter | solution.py:75
  207.4 48.2 %collective-permute-start.3 = (bf16[2048,1024]{1,0:T(8,128)(2,1)}, bf16[2048,1024]{1,0:T(8,128)(2,1)S(1)}, u32[]{:S(2)}, u32[]{:S(2)}) collective-permute-start(bf16[2048,1024]{1,0:T(8,128)(2,1)} %param.13), channel_id=1, source_target_pairs={{0,8},{8,16},{16,24},{24,0},{1,9},{9,17},{17,25},{25,1},{2,10},{10... | collective-permute-start | bytes 12582920 | tf_op jit(solution)/shard_map/ppermute | solution.py:30
  255.6 47.9 %collective-permute-start.4 = (bf16[2048,1024]{1,0:T(8,128)(2,1)S(1)}, bf16[2048,1024]{1,0:T(8,128)(2,1)S(1)}, u32[]{:S(2)}, u32[]{:S(2)}) collective-permute-start(bf16[2048,1024]{1,0:T(8,128)(2,1)S(1)} %collective-permute-done.3), channel_id=1, source_target_pairs={{0,8},{8,16},{16,24},{24,0},{1,9},{9,17},{17,25},{25,1},{2,10},{10... | collective-permute-start | bytes 12582920 | tf_op jit(solution)/shard_map/ppermute | solution.py:30
  303.5 48.1 %collective-permute-start.5 = (bf16[2048,1024]{1,0:T(8,128)(2,1)S(1)}, bf16[2048,1024]{1,0:T(8,128)(2,1)S(1)}, u32[]{:S(2)}, u32[]{:S(2)}) collective-permute-start(bf16[2048,1024]{1,0:T(8,128)(2,1)S(1)} %collective-permute-done.4), channel_id=1, source_target_pairs={{0,8},{8,16},{16,24},{24,0},{1,9},{9,17},{17,25},{25,1},{2,10},{10... | collective-permute-start | bytes 12582920 | tf_op jit(solution)/shard_map/ppermute | solution.py:30
  354.0 5.2 copy-start
  380.6 1.9 copy-start.1
Sparse Core Ops, SparseCore 0:
  12.7 107.2 all-gather.2
  206.7 143.3 all-reduce.1
  351.7 104.7 all-gather.4
  483.0 81.3 reduce-scatter.1
